TPU v7x, 32 devices: a whole 2x2x4 slice. The times are simulated.
32 devices in a mesh: gx: 32 (over z, y, x, core).
Axes of the slice: x: 2, y: 2, z: 4, core: 2. Of those that a mesh axis runs over, the one named last changes fastest.
Arguments:
- fine: bfloat16 [64, 8192, 128], P(None, 'gx'), may hold values from -6 to 6
- pattern: int32 [8, 8192], P(None, 'gx'), may hold values from 0 to 3
- stencil: bfloat16 [3, 128, 128], replicated, may hold values from -0.3125 to 0.3125
- restrict: bfloat16 [8, 4, 128, 128], replicated, may hold values from -0.5 to 0.5
- coarse_inv: bfloat16 [8, 128, 128], replicated, may hold values from -0.5 to 0.5
Outputs:
- smoothed: float32 [64, 8192, 128], P(None, 'gx')
All inputs are finite; a program needn't handle non-finite values.
Results may differ from a plain program's by a relative error of at most 0.0046.
Values may be sent and summed in bfloat16 or wider, within the bound.
A program may use at most 128 MiB of HBM per device.

v0:
```python
import jax
import jax.numpy as jnp
from jax import lax
from jax.sharding import PartitionSpec as P


def padded_2(cells, sides, width):
    for axis, dim in sides:
        count = lax.axis_size(axis)
        head = lax.slice_in_dim(cells, 0, width, axis=dim)
        tail = lax.slice_in_dim(cells, cells.shape[dim] - width, cells.shape[dim], axis=dim)
        cells = jnp.concatenate(
            [
                lax.ppermute(tail, axis, [(i, (i + 1) % count) for i in range(count)]),
                cells,
                lax.ppermute(head, axis, [((i + 1) % count, i) for i in range(count)]),
            ],
            axis=dim,
        )
    return cells


def partner_2(x, axis, apart):
    return lax.ppermute(x, axis, [(i, i ^ 1 << apart) for i in range(lax.axis_size(axis))])


def shards(fine, pattern, stencil, restrict, coarse_inv):
    devices = lax.axis_size("gx")
    vectors, blocks, width = fine.shape
    levels = restrict.shape[0]
    kind_count = restrict.shape[1]
    all_blocks = blocks * devices
    padded = padded_2(fine, (("gx", 1),), 1)
    result = jnp.einsum(
        "vic,cd->vid", padded[:, :-2], stencil[0], preferred_element_type=jnp.float32
    )
    result = result + jnp.einsum(
        "vic,cd->vid", padded[:, 1:-1], stencil[1], preferred_element_type=jnp.float32
    )
    result = result + jnp.einsum(
        "vic,cd->vid", padded[:, 2:], stencil[2], preferred_element_type=jnp.float32
    )
    kinds_row = jnp.arange(kind_count, dtype=jnp.int32)
    summed = []
    kind_maps = []
    groups = []
    counts_list = []
    for level_num in range(levels):
        coarse_num = max(all_blocks // 4 ** (level_num + 1), 1)
        span_blocks = all_blocks // coarse_num
        local_span = min(span_blocks, blocks)
        local_num = blocks // local_span
        selector = pattern[level_num][:, None] == kinds_row[None, :]
        onehot = selector.astype(jnp.bfloat16).reshape(local_num, local_span, kind_count)
        grouped = jnp.einsum(
            "vjsc,jsk->vjkc",
            fine.reshape(vectors, local_num, local_span, width),
            onehot,
            preferred_element_type=jnp.float32,
        ).astype(jnp.bfloat16)
        coarse = jnp.einsum(
            "vjkc,kcd->vjd", grouped, restrict[level_num], preferred_element_type=jnp.float32
        ) * span_blocks ** (-0.5)
        summed.append(coarse)
        kind_maps.append(pattern[level_num].reshape(local_num, local_span))
        groups.append(span_blocks // local_span)
        counts_list.append(coarse_num)
    crossing = [level_num for level_num in range(levels) if groups[level_num] > 1]
    stacked = jnp.stack([summed[level_num] for level_num in crossing])
    widest = max((groups[level_num] for level_num in crossing))
    for bit_num in range(widest.bit_length() - 1):
        first = min(
            (
                position
                for position in range(len(crossing))
                if groups[crossing[position]] > 2**bit_num
            )
        )
        upper = stacked[first:]
        partner = partner_2(upper, "gx", bit_num)
        stacked = jnp.concatenate([stacked[:first], upper + partner], axis=0)
    for position in range(len(crossing)):
        summed[crossing[position]] = stacked[position]
    for level_num in range(levels):
        rounded = summed[level_num].astype(jnp.bfloat16)
        solved = jnp.einsum(
            "vjd,de->vje", rounded, coarse_inv[level_num], preferred_element_type=jnp.float32
        ).astype(jnp.bfloat16)
        lifted = jnp.einsum(
            "vjd,kcd->vjkc", solved, restrict[level_num], preferred_element_type=jnp.float32
        )
        kind_map = kind_maps[level_num]
        for kind_num in range(kind_count):
            chosen = (kind_map == kind_num)[None, :, :, None]
            part_add = jnp.where(chosen, lifted[:, :, kind_num][:, :, None, :], jnp.float32(0.0))
            result = result + part_add.reshape(vectors, blocks, width)
    return result


def solution(mesh):
    in_specs = (P(None, "gx", None), P(None, "gx"), P(), P(), P())
    out_specs = P(None, "gx", None)
    return jax.shard_map(shards, mesh=mesh, in_specs=in_specs, out_specs=out_specs, check_vma=False)
```

profile of v0, /device:TPU:0, one launch (start us, length us, event | category | flops | bytes accessed | tf_op | source)
XLA Modules:
  0.0 162.0 jit_solution(2426209345188751192)
XLA Ops:
  0.0 1.8 %fusion.197 = (bf16[64,1,128]{2,1,0:T(2,128)(2,1)}, bf16[64,1,128]{2,1,0:T(2,128)(2,1)}) fusion(bf16[64,256,128]{2,1,0:T(8,128)(2,1)} %param.5), kind=kLoop, calls=%fused_computation.283 | loop fusion | bytes 65536 | tf_op jit(solution)/shard_map/slice | solution.py:10
  1.8 6.4 %collective-permute-start.1 = (bf16[64,1,128]{2,1,0:T(2,128)(2,1)}, bf16[64,1,128]{2,1,0:T(2,128)(2,1)}, u32[]{:S(2)}, u32[]{:S(2)}) collective-permute-start(bf16[64,1,128]{2,1,0:T(2,128)(2,1)} %get-tuple-element.44), channel_id=1, source_target_pairs={{1,0},{2,1},{3,2},{4,3},{5,4},{6,5},{7,6},{8,7},{9,8},{10,9},{11,1... | collective-permute-start | bytes 49160 | tf_op jit(solution)/shard_map/ppermute | solution.py:16
  9.2 2.8 %fusion.52 = bf16[64,4,128]{2,1,0:T(4,128)(2,1)S(1)} fusion(bf16[64,256,128]{2,1,0:T(8,128)(2,1)} %param.5, s32[256]{0:T(256)S(1)} %bitcast.462), kind=kOutput, calls=%fused_computation.82 | convolution fusion | flops 16811008 | bytes 4260864 | tf_op jit(solution)/shard_map/vjsc,jsk->vjkc/dot_general | solution.py:55
  12.1 2.8 %fusion.51 = bf16[64,4,128]{2,1,0:T(4,128)(2,1)S(1)} fusion(bf16[64,256,128]{2,1,0:T(8,128)(2,1)} %param.5, s32[256]{0:T(256)S(1)} %bitcast.461), kind=kOutput, calls=%fused_computation.81 | convolution fusion | flops 16811008 | bytes 4260864 | tf_op jit(solution)/shard_map/vjsc,jsk->vjkc/dot_general | solution.py:55
  18.5 2.8 %fusion.50 = bf16[64,4,128]{2,1,0:T(4,128)(2,1)S(1)} fusion(bf16[64,256,128]{2,1,0:T(8,128)(2,1)} %param.5, s32[256]{0:T(256)S(1)} %bitcast.458), kind=kOutput, calls=%fused_computation.80 | convolution fusion | flops 16811008 | bytes 4260864 | tf_op jit(solution)/shard_map/vjsc,jsk->vjkc/dot_general | solution.py:55
  22.5 3.0 %fusion.33 = bf16[4,4,64,128]{3,1,2,0:T(4,128)(2,1)S(1)} fusion(bf16[64,4,64,128]{3,2,1,0:T(8,128)(2,1)} %bitcast.448, s32[4,64]{1,0:T(4,128)S(1)} %eq.383), kind=kOutput, calls=%fused_computation.44 | convolution fusion | flops 16778240 | bytes 4457472 | tf_op jit(solution)/shard_map/vjsc,jsk->vjkc/dot_general | solution.py:55
  27.7 3.1 %fusion.35 = bf16[16,4,64,128]{3,1,2,0:T(4,128)(2,1)S(1)} fusion(bf16[64,16,16,128]{3,2,1,0:T(8,128)(2,1)} %bitcast.449, s32[16,16]{1,0:T(8,128)S(1)} %eq.371), kind=kOutput, calls=%fused_computation.46 | convolution fusion | flops 16778240 | bytes 5243904 | tf_op jit(solution)/shard_map/vjsc,jsk->vjkc/dot_general | solution.py:55
  31.0 1.6 %fusion.47 = bf16[64,16,128,1]{2,1,3,0:T(8,128)(2,1)S(1)} fusion(bf16[64,16,4,128]{3,0,2,1:T(8,128)(2,1)S(1)} %bitcast.456, bf16[8,4,128,128]{3,2,1,0:T(8,128)(2,1)S(1)} %copy-done.2, bf16[8,128,128]{2,1,0:T(8,128)(2,1)} %param.9), kind=kOutput, calls=%fused_computation.65 | convolution fusion | flops 168165376 | bytes 1474560 | tf_op jit(solution)/shard_map/vjd,de->vje/dot_general | solution.py:86
  33.1 1.1 slice_bitcast_fusion.7
  34.2 5.6 %fusion.39 = bf16[64,4,64,128]{3,1,2,0:T(4,128)(2,1)S(1)} fusion(bf16[64,64,4,128]{3,2,1,0:T(4,128)(2,1)} %bitcast.450, s32[64,4]{1,0:T(8,128)S(1)} %copy-done.18), kind=kOutput, calls=%fused_computation.50 | convolution fusion | flops 16778240 | bytes 8389632 | tf_op jit(solution)/shard_map/vjsc,jsk->vjkc/dot_general | solution.py:55
  39.8 3.2 %copy.82 = bf16[64,4,64,128]{3,2,1,0:T(8,128)(2,1)} copy(bf16[64,4,64,128]{3,1,2,0:T(4,128)(2,1)S(1)} %fusion.39) | data formatting | bytes 8388608 | tf_op jit(solution)/shard_map/vjsc,jsk->vjkc/dot_general | solution.py:55
  43.1 8.1 %fusion.44 = bf16[64,64,128,1]{2,1,3,0:T(8,128)(2,1)} fusion(bf16[64,64,4,128]{3,0,2,1:T(8,128)(2,1)} %bitcast.455, bf16[8,4,128,128]{3,2,1,0:T(8,128)(2,1)S(1)} %copy-done.2, bf16[8,128,128]{2,1,0:T(8,128)(2,1)} %param.9), kind=kOutput, calls=%fused_computation.60 | convolution fusion | flops 672661504 | bytes 5406720 | tf_op jit(solution)/shard_map/vjd,de->vje/dot_general | solution.py:86
  51.2 2.5 %fusion.96 = f32[64,64,4,128]{3,1,2,0:T(8,128)S(1)} fusion(bf16[64,64,128,1]{2,1,3,0:T(8,128)(2,1)} %fusion.44, bf16[8,4,128,128]{3,2,1,0:T(8,128)(2,1)S(1)} %copy-done.2), kind=kOutput, calls=%fused_computation.140 | convolution fusion | flops 536870912 | bytes 9568256 | tf_op jit(solution)/shard_map/vjd,kcd->vjkc/dot_general | solution.py:89
  53.7 3.3 %slice_bitcast_fusion.3 = (f32[64,64,128]{2,1,0:T(8,128)}, f32[64,64,128]{2,1,0:T(8,128)}, f32[64,64,128]{2,1,0:T(8,128)}, f32[64,64,128]{2,1,0:T(8,128)S(1)}) fusion(f32[64,64,4,128]{3,1,2,0:T(8,128)S(1)} %fusion.96), kind=kLoop, calls=%fused_computation.55 | loop fusion | bytes 16777216 | tf_op jit(solution)/shard_map/jit(_where)/broadcast_in_dim | solution.py:95
  56.9 1.1 copy-done.1
  58.1 4.5 %fusion.150 = f32[64,256,128]{2,1,0:T(8,128)} fusion(bf16[64,256,128]{2,1,0:T(8,128)(2,1)S(1)} %copy-done.1, bf16[3,128,128]{2,1,0:T(8,128)(2,1)S(1)} %copy-done.16), kind=kOutput, calls=%fused_computation.207 | convolution fusion | flops 536870912 | bytes 12615680 | tf_op jit(solution)/shard_map/vic,cd->vid/dot_general | solution.py:37
  65.8 5.2 %fusion.31 = f32[64,256,128]{2,1,0:T(8,128)} fusion(bf16[64,256,128]{2,1,0:T(8,128)(2,1)S(1)} %copy-done.1, bf16[64,1,128]{2,1,0:T(2,128)(2,1)} %collective-permute-done, bf16[3,128,128]{2,1,0:T(8,128)(2,1)S(1)} %copy-done.16), kind=kOutput, calls=%fused_computation.42 | convolution fusion | flops 545259520 | bytes 12632064 | tf_op jit(solution)/shard_map/vic,cd->vid/dot_general | solution.py:34
  74.0 1.8 %convolution_bitcast_fusion.4 = f32[64,1,4,128]{3,0,2,1:T(8,128)} fusion(bf16[8,4,128,128]{3,2,1,0:T(8,128)(2,1)} %param.8, bf16[8,128,128]{2,1,0:T(8,128)(2,1)} %param.9, f32[4,64,1,128]{3,1,2,0:T(8,128)S(1)} %fusion.208), kind=kOutput, calls=%fused_computation.70 | convolution fusion | flops 10493952 | bytes 311296 | tf_op jit(solution)/shard_map/vjd,kcd->vjkc/dot_general | solution.py:89
  75.8 2.3 %collective-permute-done.4 = f32[3,64,1,128]{3,1,2,0:T(8,128)} collective-permute-done((f32[3,64,1,128]{3,1,2,0:T(8,128)}, f32[3,64,1,128]{3,1,2,0:T(8,128)}, u32[]{:S(2)}, u32[]{:S(2)}) %collective-permute-start.4) | collective-permute-done | bytes 98336 | tf_op jit(solution)/shard_map/ppermute | solution.py:24
  79.6 1.5 slice_bitcast_fusion.27
  81.0 2.7 %collective-permute-done.5 = f32[3,64,1,128]{3,1,2,0:T(8,128)S(1)} collective-permute-done((f32[3,64,1,128]{3,1,2,0:T(8,128)S(1)}, f32[3,64,1,128]{3,1,2,0:T(8,128)S(1)}, u32[]{:S(2)}, u32[]{:S(2)}) %collective-permute-start.5) | collective-permute-done | bytes 98336 | tf_op jit(solution)/shard_map/ppermute | solution.py:24
  84.4 1.8 %convolution_bitcast_fusion.3 = f32[64,1,4,128]{3,0,2,1:T(8,128)} fusion(bf16[8,4,128,128]{3,2,1,0:T(8,128)(2,1)} %param.8, bf16[8,128,128]{2,1,0:T(8,128)(2,1)} %param.9, f32[3,64,1,128]{3,1,2,0:T(8,128)S(1)} %add.142), kind=kOutput, calls=%fused_computation.69 | convolution fusion | flops 10493952 | bytes 311296 | tf_op jit(solution)/shard_map/vjd,kcd->vjkc/dot_general | solution.py:89
  86.2 2.8 %collective-permute-start.6 = (f32[2,64,1,128]{3,1,2,0:T(8,128)}, f32[2,64,1,128]{3,1,2,0:T(8,128)S(1)}, u32[]{:S(2)}, u32[]{:S(2)}) collective-permute-start(f32[2,64,1,128]{3,1,2,0:T(8,128)} %slice.330), channel_id=1, source_target_pairs={{0,16},{1,17},{2,18},{3,19},{4,20},{5,21},{6,22},{7,23},{8,24},{9,... | collective-permute-start | bytes 196616 | tf_op jit(solution)/shard_map/ppermute | solution.py:24
  89.0 1.5 slice_bitcast_fusion.23
  92.2 1.2 convolution_bitcast_fusion.1
  93.4 1.9 %convolution_bitcast_fusion.2 = f32[64,1,4,128]{3,0,2,1:T(8,128)} fusion(bf16[8,4,128,128]{3,2,1,0:T(8,128)(2,1)} %param.8, bf16[8,128,128]{2,1,0:T(8,128)(2,1)} %param.9, bf16[2,64,1,128]{3,1,2,0:T(8,128)(2,1)} %add_convert_fusion), kind=kOutput, calls=%fused_computation.68 | convolution fusion | flops 10493952 | bytes 311296 | tf_op jit(solution)/shard_map/vjd,kcd->vjkc/dot_general | solution.py:89
  95.3 1.5 slice_bitcast_fusion.15
  96.8 6.6 %broadcast_in_dim.552 = f32[64,64,4,128]{3,2,1,0:T(4,128)} broadcast(f32[64,64,128]{2,1,0:T(8,128)} %get-tuple-element.40), dimensions={0,1,3} | broadcast | bytes 10485760 | tf_op jit(solution)/shard_map/jit(_where)/broadcast_in_dim | solution.py:95
  103.4 6.5 %broadcast_in_dim.565 = f32[64,64,4,128]{3,2,1,0:T(4,128)} broadcast(f32[64,64,128]{2,1,0:T(8,128)} %get-tuple-element.41), dimensions={0,1,3} | broadcast | bytes 10485760 | tf_op jit(solution)/shard_map/jit(_where)/broadcast_in_dim | solution.py:95
  109.9 6.4 %broadcast_in_dim.561 = f32[64,64,4,128]{3,2,1,0:T(4,128)} broadcast(f32[64,64,128]{2,1,0:T(8,128)} %get-tuple-element.42), dimensions={0,1,3} | broadcast | bytes 10485760 | tf_op jit(solution)/shard_map/jit(_where)/broadcast_in_dim | solution.py:95
  116.3 4.8 %broadcast_in_dim.557 = f32[64,64,4,128]{3,2,1,0:T(4,128)} broadcast(f32[64,64,128]{2,1,0:T(8,128)S(1)} %get-tuple-element.43), dimensions={0,1,3} | broadcast | bytes 10485760 | tf_op jit(solution)/shard_map/jit(_where)/broadcast_in_dim | solution.py:95
  121.1 40.7 %fusion.20 = f32[64,256,128]{2,1,0:T(8,128)} fusion(f32[64,256,128]{2,1,0:T(8,128)} %bitcast.452, f32[64,256,128]{2,1,0:T(8,128)} %bitcast.453, f32[64,256,128]{2,1,0:T(8,128)} %bitcast.454, f32[64,256,128]{2,1,0:T(8,128)} %bitcast.451, f32[64,256,128]{2,1,0:T(8,128)} %fusion.31, f32[64,256,128]{2,1,0:T(8,128)} %fusion.150, ...), kind=kOutput, calls=%fused_computation.21 | convolution fusion | flops 683671552 | bytes 66272256 | tf_op jit(solution)/shard_map/vic,cd->vid/dot_general | solution.py:40
  (79 shorter events, 18.5 us)
Async XLA Ops:
  0.0 15.2 %copy-start = (bf16[64,256,128]{2,1,0:T(8,128)(2,1)S(1)}, bf16[64,256,128]{2,1,0:T(8,128)(2,1)}, u32[]{:S(2)}) copy-start(bf16[64,256,128]{2,1,0:T(8,128)(2,1)} %param.5) | copy-start | bytes 12582916
  0.0 14.9 %copy-start.2 = (bf16[8,4,128,128]{3,2,1,0:T(8,128)(2,1)S(1)}, bf16[8,4,128,128]{3,2,1,0:T(8,128)(2,1)}, u32[]{:S(2)}) copy-start(bf16[8,4,128,128]{3,2,1,0:T(8,128)(2,1)} %param.8) | copy-start | bytes 3145732
  1.8 95.0 %collective-permute-start.1 = (bf16[64,1,128]{2,1,0:T(2,128)(2,1)}, bf16[64,1,128]{2,1,0:T(2,128)(2,1)}, u32[]{:S(2)}, u32[]{:S(2)}) collective-permute-start(bf16[64,1,128]{2,1,0:T(2,128)(2,1)} %get-tuple-element.44), channel_id=1, source_target_pairs={{1,0},{2,1},{3,2},{4,3},{5,4},{6,5},{7,6},{8,7},{9,8},{10,9},{11,1... | collective-permute-start | bytes 49160 | tf_op jit(solution)/shard_map/ppermute | solution.py:16
  8.2 57.6 %collective-permute-start = (bf16[64,1,128]{2,1,0:T(2,128)(2,1)}, bf16[64,1,128]{2,1,0:T(2,128)(2,1)}, u32[]{:S(2)}, u32[]{:S(2)}) collective-permute-start(bf16[64,1,128]{2,1,0:T(2,128)(2,1)} %get-tuple-element.45), channel_id=1, source_target_pairs={{0,1},{1,2},{2,3},{3,4},{4,5},{5,6},{6,7},{7,8},{8,9},{9,10},{10,1... | collective-permute-start | bytes 49160 | tf_op jit(solution)/shard_map/ppermute | solution.py:14
  15.1 1.8 %copy-start.8 = (f32[1,64,1,128]{3,1,2,0:T(8,128)}, f32[1,64,1,128]{3,1,2,0:T(8,128)S(1)}, u32[]{:S(2)}) copy-start(f32[1,64,1,128]{3,1,2,0:T(8,128)S(1)} %fusion.60) | copy-start | bytes 98308
  15.2 2.3 %copy-start.10 = (f32[1,64,1,128]{3,1,2,0:T(8,128)}, f32[1,64,1,128]{3,1,2,0:T(8,128)S(1)}, u32[]{:S(2)}) copy-start(f32[1,64,1,128]{3,1,2,0:T(8,128)S(1)} %fusion.62) | copy-start | bytes 98308
  16.1 1.5 copy-start.12
  16.9 0.7 copy-start.14
  17.6 48.1 %collective-permute-start.2 = (f32[4,64,1,128]{3,1,2,0:T(8,128)}, f32[4,64,1,128]{3,1,2,0:T(8,128)S(1)}, u32[]{:S(2)}, u32[]{:S(2)}) collective-permute-start(f32[4,64,1,128]{3,1,2,0:T(8,128)} %pad_maximum_fusion.6), channel_id=1, source_target_pairs={{0,1},{1,0},{2,3},{3,2},{4,5},{5,4},{6,7},{7,6},{8,9},{9,8},{10,11... | collective-permute-start | bytes 393224 | tf_op jit(solution)/shard_map/ppermute | solution.py:24
  27.6 6.6 %copy-start.18 = (s32[64,4]{1,0:T(8,128)S(1)}, s32[64,4]{1,0:T(8,128)}, u32[]{:S(2)}) copy-start(s32[64,4]{1,0:T(8,128)} %eq.356) | copy-start | bytes 3076
  53.6 4.4 %copy-start.1 = (bf16[64,256,128]{2,1,0:T(8,128)(2,1)S(1)}, bf16[64,256,128]{2,1,0:T(8,128)(2,1)}, u32[]{:S(2)}) copy-start(bf16[64,256,128]{2,1,0:T(8,128)(2,1)} %param.5) | copy-start | bytes 12582916
  53.6 4.4 %copy-start.16 = (bf16[3,128,128]{2,1,0:T(8,128)(2,1)S(1)}, bf16[3,128,128]{2,1,0:T(8,128)(2,1)}, u32[]{:S(2)}) copy-start(bf16[3,128,128]{2,1,0:T(8,128)(2,1)} %param.7) | copy-start | bytes 294916
  58.0 5.3 %copy-start.7 = (f32[64,4,128]{2,0,1:T(8,128)S(1)}, f32[64,4,128]{2,0,1:T(8,128)}, u32[]{:S(2)}) copy-start(f32[64,4,128]{2,0,1:T(8,128)} %get-tuple-element.51) | copy-start | bytes 393220
  58.0 5.4 %copy-start.6 = (f32[64,4,128]{2,0,1:T(8,128)S(1)}, f32[64,4,128]{2,0,1:T(8,128)}, u32[]{:S(2)}) copy-start(f32[64,4,128]{2,0,1:T(8,128)} %get-tuple-element.52) | copy-start | bytes 393220
  58.0 6.1 %copy-start.5 = (f32[64,4,128]{2,0,1:T(8,128)S(1)}, f32[64,4,128]{2,0,1:T(8,128)}, u32[]{:S(2)}) copy-start(f32[64,4,128]{2,0,1:T(8,128)} %get-tuple-element.53) | copy-start | bytes 393220
  58.0 6.8 %copy-start.17 = (s32[8,256]{1,0:T(8,128)S(1)}, s32[8,256]{1,0:T(8,128)}, u32[]{:S(2)}) copy-start(s32[8,256]{1,0:T(8,128)} %param.6) | copy-start | bytes 24580
  58.1 7.6 %copy-start.9 = (f32[1,64,1,128]{3,1,2,0:T(8,128)S(1)}, f32[1,64,1,128]{3,1,2,0:T(8,128)}, u32[]{:S(2)}) copy-start(f32[1,64,1,128]{3,1,2,0:T(8,128)} %copy-done.8) | copy-start | bytes 98308
  58.1 7.6 %copy-start.11 = (f32[1,64,1,128]{3,1,2,0:T(8,128)S(1)}, f32[1,64,1,128]{3,1,2,0:T(8,128)}, u32[]{:S(2)}) copy-start(f32[1,64,1,128]{3,1,2,0:T(8,128)} %copy-done.10) | copy-start | bytes 98308
  58.1 7.5 %copy-start.13 = (f32[1,64,1,128]{3,1,2,0:T(8,128)S(1)}, f32[1,64,1,128]{3,1,2,0:T(8,128)}, u32[]{:S(2)}) copy-start(f32[1,64,1,128]{3,1,2,0:T(8,128)} %copy-done.12) | copy-start | bytes 98308
  58.1 7.5 %copy-start.15 = (f32[1,64,1,128]{3,1,2,0:T(8,128)S(1)}, f32[1,64,1,128]{3,1,2,0:T(8,128)}, u32[]{:S(2)}) copy-start(f32[1,64,1,128]{3,1,2,0:T(8,128)} %copy-done.14) | copy-start | bytes 98308
  65.6 5.4 %copy-start.4 = (f32[4,64,1,128]{3,1,2,0:T(8,128)}, f32[4,64,1,128]{3,1,2,0:T(8,128)S(1)}, u32[]{:S(2)}) copy-start(f32[4,64,1,128]{3,1,2,0:T(8,128)S(1)} %collective-permute-done.2) | copy-start | bytes 393220
  65.7 6.0 %collective-permute-start.3 = (f32[4,64,1,128]{3,1,2,0:T(8,128)S(1)}, f32[4,64,1,128]{3,1,2,0:T(8,128)S(1)}, u32[]{:S(2)}, u32[]{:S(2)}) collective-permute-start(f32[4,64,1,128]{3,1,2,0:T(8,128)S(1)} %fusion.196), channel_id=1, source_target_pairs={{0,2},{1,3},{2,0},{3,1},{4,6},{5,7},{6,4},{7,5},{8,10},{9,11},{10,... | collective-permute-start | bytes 393224 | tf_op jit(solution)/shard_map/ppermute | solution.py:24
  73.2 4.9 %collective-permute-start.4 = (f32[3,64,1,128]{3,1,2,0:T(8,128)}, f32[3,64,1,128]{3,1,2,0:T(8,128)}, u32[]{:S(2)}, u32[]{:S(2)}) collective-permute-start(f32[3,64,1,128]{3,1,2,0:T(8,128)} %slice.324), channel_id=1, source_target_pairs={{0,4},{1,5},{2,6},{3,7},{4,0},{5,1},{6,2},{7,3},{8,12},{9,13},{10,... | collective-permute-start | bytes 294920 | tf_op jit(solution)/shard_map/ppermute | solution.py:24
  79.1 4.7 %collective-permute-start.5 = (f32[3,64,1,128]{3,1,2,0:T(8,128)S(1)}, f32[3,64,1,128]{3,1,2,0:T(8,128)S(1)}, u32[]{:S(2)}, u32[]{:S(2)}) collective-permute-start(f32[3,64,1,128]{3,1,2,0:T(8,128)S(1)} %slice_add_fusion), channel_id=1, source_target_pairs={{0,8},{1,9},{2,10},{3,11},{4,12},{5,13},{6,14},{7,15},{8,0},{9,1},... | collective-permute-start | bytes 294920 | tf_op jit(solution)/shard_map/ppermute | solution.py:24
  86.2 5.4 %collective-permute-start.6 = (f32[2,64,1,128]{3,1,2,0:T(8,128)}, f32[2,64,1,128]{3,1,2,0:T(8,128)S(1)}, u32[]{:S(2)}, u32[]{:S(2)}) collective-permute-start(f32[2,64,1,128]{3,1,2,0:T(8,128)} %slice.330), channel_id=1, source_target_pairs={{0,16},{1,17},{2,18},{3,19},{4,20},{5,21},{6,22},{7,23},{8,24},{9,... | collective-permute-start | bytes 196616 | tf_op jit(solution)/shard_map/ppermute | solution.py:24
  109.9 11.2 %copy-start.3 = (f32[64,4,128]{2,1,0:T(4,128)S(1)}, f32[64,4,128]{2,1,0:T(4,128)}, u32[]{:S(2)}) copy-start(f32[64,4,128]{2,1,0:T(4,128)} %copy.16) | copy-start | bytes 393220
where the time goes:
time: 163 us; the launch traced here: 162 us
  matrix products  94.4 us (58%)
  local copies, waits for them, and re-layouts  45.9 us (28%)
  starting transfers between devices  10.6 us (7%)
  waiting for transfers between devices  6.77 us (4%)
  other arithmetic  3.87 us (2%)
    dot_general x1, matrix products, shards(): jnp.einsum('vic,cd->vid', padded[:, 2:], stencil[2], preferred_element_ty...  40.7 us
    broadcast_in_dim x15, local copies, waits for them, and re-layouts, shards(): jnp.where(chosen, lifted[:, :, kind_num][:, :, None, :], jnp.float32(0.0))  36.2 us
    dot_general x8, matrix products, shards(): jnp.einsum('vjsc,jsk->vjkc', fine.reshape(vectors, local_num, local_span,...  21.4 us
    dot_general x8, matrix products, shards(): jnp.einsum('vjd,kcd->vjkc', solved, restrict[level_num], preferred_elemen...  10.9 us
    dot_general x3, matrix products, shards(): jnp.einsum('vjd,de->vje', rounded, coarse_inv[level_num], preferred_eleme...  10.8 us
    ppermute x5, waiting for transfers between devices, partner_2(): lax.ppermute(x, axis, [(i, i ^ 1 << apart) for i in range(lax.axis_size(a...  6.76 us
    ppermute x1, starting transfers between devices, padded_2(): lax.ppermute(head, axis, [((i + 1) % count, i) for i in range(count)])  6.4 us
    dot_general x1, matrix products, shards(): jnp.einsum('vic,cd->vid', padded[:, :-2], stencil[0], preferred_element_t...  5.23 us
  transfers between devices with their start and end apart: 7, of which 4 were waited for; matrix products, arithmetic and copies ran while one was open for 47% of the time, Pallas kernels for 0%

commit v1 on v0

v1 whole, which is shorter than its diff:
```python
import functools

import jax
import jax.numpy as jnp
from jax import lax
from jax.experimental import pallas as pl
from jax.experimental.pallas import tpu as pltpu
from jax.sharding import PartitionSpec as P

MESH = pl.DeviceIdType.MESH
F32 = jnp.float32
BF16 = jnp.bfloat16
TILE = 16
VMEM_LIMIT = 40 * 2**20


def round_up(value, unit):
    return -(-value // unit) * unit


class Plan:
    def __init__(self, devices, vectors, blocks, width, levels, kinds):
        self.devices, self.vectors, self.blocks = devices, vectors, blocks
        self.width, self.levels, self.kinds = width, levels, kinds
        all_blocks = devices * blocks
        self.spans, self.local_spans, self.counts, self.groups = [], [], [], []
        for level in range(levels):
            span = all_blocks // max(all_blocks // 4 ** (level + 1), 1)
            local = min(span, blocks)
            self.spans.append(span)
            self.local_spans.append(local)
            self.counts.append(blocks // local)
            self.groups.append(span // local)
        self.narrow = [l for l in range(levels) if self.counts[l] > 1]
        self.wide = [l for l in range(levels) if self.counts[l] == 1]
        self.crossing = [l for l in range(levels) if self.groups[l] > 1]
        self.padded = {l: round_up(self.counts[l], TILE) for l in self.narrow}
        self.offsets, at = {}, 0
        for l in self.narrow:
            self.offsets[l] = at
            at += kinds * self.padded[l]
        self.narrow_rows = at
        self.wide_used = len(self.wide) * kinds + 2
        self.wide_rows = round_up(self.wide_used, TILE)


def wide_rows_onehot(plan, pattern, rows_axis):
    shape = (plan.wide_rows, plan.blocks) if rows_axis == 0 else (plan.blocks, plan.wide_rows)
    row = lax.broadcasted_iota(jnp.int32, shape, rows_axis)
    block = lax.broadcasted_iota(jnp.int32, shape, 1 - rows_axis)
    base = len(plan.wide) * plan.kinds
    hit = ((row == base) & (block == 0)) | ((row == base + 1) & (block == plan.blocks - 1))
    for position, level in enumerate(plan.wide):
        kinds = pattern[level : level + 1, :] if rows_axis == 0 else pattern[:, level : level + 1]
        first = position * plan.kinds
        inside = (row >= first) & (row < first + plan.kinds)
        hit = hit | (inside & (row - first == kinds))
    return hit.astype(F32).astype(BF16)


def narrow_onehot(plan, pattern, level, rows_axis):
    padded = plan.padded[level]
    rows = plan.kinds * padded
    shape = (rows, plan.blocks) if rows_axis == 0 else (plan.blocks, rows)
    row = lax.broadcasted_iota(jnp.int32, shape, rows_axis)
    block = lax.broadcasted_iota(jnp.int32, shape, 1 - rows_axis)
    kinds = pattern[level : level + 1, :] if rows_axis == 0 else pattern[:, level : level + 1]
    target = kinds * padded + block // plan.local_spans[level]
    return (row == target).astype(F32).astype(BF16)


def pair_of(ref, first):
    return jnp.concatenate([ref[first], ref[first + 1]], axis=1)


def wide_kernel(plan, chunk, pattern_ref, fine_ref, restrict_ref, coarse_ref, halo_ref, onehot, grouped, rows):
    step = pl.program_id(0)
    width = plan.width

    @pl.when(step == 0)
    def _():
        onehot[...] = wide_rows_onehot(plan, pattern_ref[...], 0)

    for first in range(0, chunk, 2):
        both = jnp.dot(onehot[...], pair_of(fine_ref, first), preferred_element_type=F32)
        grouped[first] = both[:, :width]
        grouped[first + 1] = both[:, width:]
    here = pl.ds(pl.multiple_of(step * chunk, chunk), chunk)
    for row in range(plan.wide_used):
        rows[row, here, :] = grouped[:, row, :].astype(BF16)

    @pl.when(step == pl.num_programs(0) - 1)
    def _():
        for position, level in enumerate(plan.wide):
            first = position * plan.kinds
            joined = jnp.concatenate([rows[first + kind] for kind in range(plan.kinds)], axis=1)
            coarse = jnp.dot(joined, restrict_ref[level], preferred_element_type=F32)
            coarse_ref[position] = (coarse * plan.spans[level] ** (-0.5)).astype(BF16)
        base = len(plan.wide) * plan.kinds
        halo_ref[0] = rows[base]
        halo_ref[1] = rows[base + 1]


def exchange_kernel(plan, coarse_ref, halo_ref, sums_ref, beside_ref, *scratch):
    (from_group, to_column, from_column, to_group, back, group_send, group_recv,
     column_send, column_recv, back_send, back_recv, halo_send, halo_recv) = scratch
    devices = plan.devices
    near = plan.groups[plan.crossing[0]]
    far = devices // near
    local = len(plan.wide) - len(plan.crossing)
    crossing = len(plan.crossing)
    part = plan.vectors // near
    me = lax.axis_index("gx")
    mine = lax.rem(me, near)
    place = me // near

    def group_peer(apart):
        return place * near + lax.rem(mine + apart, near)

    def column_peer(apart):
        return lax.rem(place + apart, far) * near + mine

    nexts = lax.rem(me + 1, devices)
    previous = lax.rem(me + devices - 1, devices)
    barrier = pltpu.get_barrier_semaphore()
    peers = [group_peer(a) for a in range(1, near)] + [column_peer(a) for a in range(1, far)] + [nexts, previous]
    for peer in peers:
        pl.semaphore_signal(barrier, inc=1, device_id=(peer,), device_id_type=MESH)
    pl.semaphore_wait(barrier, len(peers))

    def part_of(index):
        return pl.ds(pl.multiple_of(index * part, part), part)

    copies = []
    for apart in range(1, near):
        theirs = lax.rem(mine + apart, near)
        copies.append(pltpu.make_async_remote_copy(
            src_ref=coarse_ref.at[pl.ds(local, crossing), part_of(theirs), :],
            dst_ref=from_group.at[apart],
            send_sem=group_send.at[apart], recv_sem=group_recv.at[apart],
            device_id=(group_peer(apart),), device_id_type=MESH))
    halo_copies = []
    for side, peer in ((0, previous), (1, nexts)):
        halo_copies.append(pltpu.make_async_remote_copy(
            src_ref=halo_ref.at[side], dst_ref=beside_ref.at[1 - side],
            send_sem=halo_send.at[side], recv_sem=halo_recv.at[1 - side],
            device_id=(peer,), device_id_type=MESH))
    for copy in copies + halo_copies:
        copy.start()
    total = coarse_ref[pl.ds(local, crossing), part_of(mine), :].astype(F32)
    for apart, copy in enumerate(copies, 1):
        copy.wait_recv()
        total = total + from_group[apart].astype(F32)
    to_column[...] = total.astype(BF16)

    column_copies = []
    for apart in range(1, far):
        column_copies.append(pltpu.make_async_remote_copy(
            src_ref=to_column.at[pl.ds(1, crossing - 1)], dst_ref=from_column.at[apart],
            send_sem=column_send.at[apart], recv_sem=column_recv.at[apart],
            device_id=(column_peer(apart),), device_id_type=MESH))
    for copy in column_copies:
        copy.start()
    sums = [total[index] for index in range(crossing)]
    for apart, copy in enumerate(column_copies, 1):
        copy.wait_recv()
        source = lax.rem(place + far - apart, far)
        for index in range(1, crossing):
            reach = plan.groups[plan.crossing[index]] // near
            keep = (source // reach == place // reach).astype(F32)
            sums[index] = sums[index] + keep * from_column[apart, index - 1].astype(F32)
    for index in range(crossing):
        to_group[index] = sums[index].astype(BF16)

    back_copies = []
    for apart in range(1, near):
        back_copies.append(pltpu.make_async_remote_copy(
            src_ref=to_group, dst_ref=back.at[apart],
            send_sem=back_send.at[apart], recv_sem=back_recv.at[apart],
            device_id=(group_peer(apart),), device_id_type=MESH))
    for copy in back_copies:
        copy.start()
    for index in range(local):
        sums_ref[index] = coarse_ref[index]
    sums_ref[pl.ds(local, crossing), part_of(mine), :] = to_group[...]
    for apart, copy in enumerate(back_copies, 1):
        copy.wait_recv()
        source = lax.rem(mine + near - apart, near)
        sums_ref[pl.ds(local, crossing), part_of(source), :] = back[apart]
    for copy in halo_copies:
        copy.wait_recv()
    for copy in copies + halo_copies + column_copies + back_copies:
        copy.wait_send()


def narrow_kernel(plan, chunk, pattern_ref, fine_ref, restrict_ref, inverse_ref, lifted_ref, onehot, grouped):
    width = plan.width

    @pl.when(pl.program_id(0) == 0)
    def _():
        for level in plan.narrow:
            rows = pl.ds(plan.offsets[level], plan.kinds * plan.padded[level])
            onehot[rows, :] = narrow_onehot(plan, pattern_ref[...], level, 0)

    for first in range(0, chunk, 2):
        both = jnp.dot(onehot[...], pair_of(fine_ref, first), preferred_element_type=F32).astype(BF16)
        grouped[first] = both[:, :width]
        grouped[first + 1] = both[:, width:]
    for level in plan.narrow:
        padded = plan.padded[level]
        slices = [pl.ds(plan.offsets[level] + kind * padded, padded) for kind in range(plan.kinds)]
        joined = jnp.concatenate(
            [grouped[:, rows, :].reshape(chunk * padded, width) for rows in slices], axis=1)
        coarse = jnp.dot(joined, restrict_ref[level], preferred_element_type=F32)
        rounded = (coarse * plan.spans[level] ** (-0.5)).astype(BF16)
        solved = jnp.dot(rounded, inverse_ref[level], preferred_element_type=F32).astype(BF16)
        lifted = lax.dot_general(
            solved, restrict_ref[level], (((1,), (1,)), ((), ())), preferred_element_type=F32).astype(BF16)
        for kind, rows in enumerate(slices):
            lifted_ref[:, rows, :] = lifted[:, kind * width : (kind + 1) * width].reshape(chunk, padded, width)


def final_kernel(plan, chunk, pattern_ref, sums_ref, beside_ref, stencil_ref, restrict_ref, inverse_ref,
                 fine_ref, lifted_ref, out_ref, spread, wide_lifted, before, after):
    step = pl.program_id(0)
    width, blocks, kinds = plan.width, plan.blocks, plan.kinds

    @pl.when(step == 0)
    def _():
        turned = pattern_ref[...].T
        for level in plan.narrow:
            columns = pl.ds(plan.offsets[level], kinds * plan.padded[level])
            spread[:, columns] = narrow_onehot(plan, turned, level, 1)
        spread[:, pl.ds(plan.narrow_rows, plan.wide_rows)] = wide_rows_onehot(plan, turned, 1)
        for position, level in enumerate(plan.wide):
            solved = jnp.dot(sums_ref[position], inverse_ref[level], preferred_element_type=F32).astype(BF16)
            lifted = lax.dot_general(
                solved, restrict_ref[level], (((1,), (1,)), ((), ())), preferred_element_type=F32)
            for kind in range(kinds):
                wide_lifted[:, position * kinds + kind, :] = lifted[:, kind * width : (kind + 1) * width]
        base = len(plan.wide) * kinds
        wide_lifted[:, base, :] = jnp.dot(beside_ref[0], stencil_ref[0], preferred_element_type=F32)
        wide_lifted[:, base + 1, :] = jnp.dot(beside_ref[1], stencil_ref[2], preferred_element_type=F32)
        for row in range(plan.wide_used, plan.wide_rows):
            wide_lifted[:, row, :] = jnp.zeros((plan.vectors, width), F32)
        for slot in range(2):
            before[slot, pl.ds(0, 8), :] = jnp.zeros((8, width), F32)
            after[slot, pl.ds(blocks, 8), :] = jnp.zeros((8, width), F32)

    stencils = jnp.concatenate([stencil_ref[0], stencil_ref[1], stencil_ref[2]], axis=1)
    for first in range(0, chunk, 2):
        tables = []
        for slot in range(2):
            vector = step * chunk + first + slot
            tables.append(jnp.concatenate([lifted_ref[first + slot], wide_lifted[vector].astype(BF16)], axis=0))
        both = jnp.dot(spread[...], jnp.concatenate(tables, axis=1), preferred_element_type=F32)
        for slot in range(2):
            three = jnp.dot(fine_ref[first + slot], stencils, preferred_element_type=F32)
            before[slot, pl.ds(8, blocks), :] = three[:, :width]
            after[slot, pl.ds(0, blocks), :] = three[:, 2 * width :]
            result = both[:, slot * width : (slot + 1) * width] + three[:, width : 2 * width]
            result = result + before[slot, pl.ds(7, blocks), :]
            out_ref[first + slot] = result + after[slot, pl.ds(1, blocks), :]


def whole(ndim_shape):
    return pl.BlockSpec(ndim_shape, lambda *_: (0,) * len(ndim_shape))


def shards(fine, pattern, stencil, restrict, coarse_inv):
    devices = lax.axis_size("gx")
    vectors, blocks, width = fine.shape
    levels, kinds = restrict.shape[:2]
    plan = Plan(devices, vectors, blocks, width, levels, kinds)
    stacked = restrict.reshape(levels, kinds * width, width)
    wide_count = len(plan.wide)
    params = pltpu.CompilerParams(dimension_semantics=("arbitrary",), vmem_limit_bytes=VMEM_LIMIT)

    chunk = 16
    fine_spec = pl.BlockSpec((chunk, blocks, width), lambda i: (i, 0, 0))
    coarse, halo = pl.pallas_call(
        functools.partial(wide_kernel, plan, chunk),
        grid=(vectors // chunk,),
        out_shape=(jax.ShapeDtypeStruct((wide_count, vectors, width), BF16),
                   jax.ShapeDtypeStruct((2, vectors, width), BF16)),
        in_specs=[whole(pattern.shape), fine_spec, whole(stacked.shape)],
        out_specs=(whole((wide_count, vectors, width)), whole((2, vectors, width))),
        scratch_shapes=[
            pltpu.VMEM((plan.wide_rows, blocks), BF16),
            pltpu.VMEM((chunk, plan.wide_rows, width), F32),
            pltpu.VMEM((plan.wide_used, vectors, width), BF16),
        ],
        compiler_params=params,
        name="wide",
    )(pattern, fine, stacked)

    near = plan.groups[plan.crossing[0]]
    far = devices // near
    crossing = len(plan.crossing)
    part = vectors // near
    vmem = pl.BlockSpec(memory_space=pltpu.VMEM)
    dma = pltpu.SemaphoreType.DMA
    sums, beside = pl.pallas_call(
        functools.partial(exchange_kernel, plan),
        out_shape=(jax.ShapeDtypeStruct(coarse.shape, BF16), jax.ShapeDtypeStruct(halo.shape, BF16)),
        in_specs=[vmem, vmem],
        out_specs=(vmem, vmem),
        scratch_shapes=[
            pltpu.VMEM((near, crossing, part, width), BF16),
            pltpu.VMEM((crossing, part, width), BF16),
            pltpu.VMEM((far, crossing - 1, part, width), BF16),
            pltpu.VMEM((crossing, part, width), BF16),
            pltpu.VMEM((near, crossing, part, width), BF16),
            dma((near,)), dma((near,)), dma((far,)), dma((far,)), dma((near,)), dma((near,)), dma((2,)), dma((2,)),
        ],
        compiler_params=pltpu.CompilerParams(collective_id=0, has_side_effects=True),
        name="exchange",
    )(coarse, halo)

    lifted = pl.pallas_call(
        functools.partial(narrow_kernel, plan, chunk),
        grid=(vectors // chunk,),
        out_shape=jax.ShapeDtypeStruct((vectors, plan.narrow_rows, width), BF16),
        in_specs=[whole(pattern.shape), fine_spec, whole(stacked.shape), whole(coarse_inv.shape)],
        out_specs=pl.BlockSpec((chunk, plan.narrow_rows, width), lambda i: (i, 0, 0)),
        scratch_shapes=[
            pltpu.VMEM((plan.narrow_rows, blocks), BF16),
            pltpu.VMEM((chunk, plan.narrow_rows, width), BF16),
        ],
        compiler_params=params,
        name="narrow",
    )(pattern, fine, stacked, coarse_inv)

    last = 8
    return pl.pallas_call(
        functools.partial(final_kernel, plan, last),
        grid=(vectors // last,),
        out_shape=jax.ShapeDtypeStruct(fine.shape, F32),
        in_specs=[
            whole(pattern.shape), whole(sums.shape), whole(beside.shape), whole(stencil.shape),
            whole(stacked.shape), whole(coarse_inv.shape),
            pl.BlockSpec((last, blocks, width), lambda i: (i, 0, 0)),
            pl.BlockSpec((last, plan.narrow_rows, width), lambda i: (i, 0, 0)),
        ],
        out_specs=pl.BlockSpec((last, blocks, width), lambda i: (i, 0, 0)),
        scratch_shapes=[
            pltpu.VMEM((blocks, plan.narrow_rows + plan.wide_rows), BF16),
            pltpu.VMEM((vectors, plan.wide_rows, width), F32),
            pltpu.VMEM((2, blocks + 8, width), F32),
            pltpu.VMEM((2, blocks + 8, width), F32),
        ],
        compiler_params=params,
        name="final",
    )(pattern, sums, beside, stencil, stacked, coarse_inv, fine, lifted)


def solution(mesh):
    in_specs = (P(None, "gx", None), P(None, "gx"), P(), P(), P())
    out_specs = P(None, "gx", None)
    return jax.shard_map(shards, mesh=mesh, in_specs=in_specs, out_specs=out_specs, check_vma=False)
```

time: 163 us -> 48.5 us (0.30)
  matrix products: 94.4 us -> 0 us
  Pallas kernels: 0 us -> 37.6 us
  local copies, waits for them, and re-layouts: 45.9 us -> 10.4 us
  starting transfers between devices: 10.6 us -> 0 us
  waiting for transfers between devices: 6.77 us -> 0 us
  other arithmetic: 3.87 us -> 0 us
    dot_general x27 -> x0, matrix products: 94.4 us -> none  [the longest x1 40.7 us: shards(): jnp.einsum('vic,cd->vid', padded[:, 2:], stencil[2], preferred_element_ty...]
    pallas_call x0 -> x4, Pallas kernels: none -> 37.6 us  [the longest x1 16.8 us: shards(): pl.pallas_call(functools.partial(exchange_kernel, plan), out_shape=(jax.S...]
    broadcast_in_dim x15 -> x0, local copies, waits for them, and re-layouts: 36.2 us -> none  [shards(): jnp.where(chosen, lifted[:, :, kind_num][:, :, None, :], jnp.float32(0.0))]
    ppermute x7 -> x0, starting transfers between devices: 10.6 us -> none  [the longest x1 6.4 us: padded_2(): lax.ppermute(head, axis, [((i + 1) % count, i) for i in range(count)])]
    unnamed x39 -> x26, local copies, waits for them, and re-layouts: 1.24 us -> 10.4 us
    ppermute x7 -> x0, waiting for transfers between devices: 6.77 us -> none  [the longest x5 6.76 us: partner_2(): lax.ppermute(x, axis, [(i, i ^ 1 << apart) for i in range(lax.axis_size(a...]
    slice x4 -> x0, local copies, waits for them, and re-layouts: 4.06 us -> none  [the longest x1 1.79 us: padded_2(): head = lax.slice_in_dim(cells, 0, width, axis=dim)]
    dot_general x2 -> x0, local copies, waits for them, and re-layouts: 3.5 us -> none  [shards(): jnp.einsum('vjsc,jsk->vjkc', fine.reshape(vectors, local_num, local_span,...]
  transfers between devices with their start and end apart: 7 -> 0, of which waited for: 4 -> 0; matrix products, arithmetic and copies ran while one was open for 47% -> 0% of each run, Pallas kernels for 0% -> 0%
where the time goes in v1:
time: 48.5 us; the launch traced here: 48.1 us
  Pallas kernels  37.6 us (78%)
  local copies, waits for them, and re-layouts  10.4 us (21%)
    pallas_call x1, Pallas kernels, shards(): pl.pallas_call(functools.partial(exchange_kernel, plan), out_shape=(jax.S...  16.8 us
    unnamed x26, local copies, waits for them, and re-layouts  10.4 us
    pallas_call x1, Pallas kernels, shards(): pl.pallas_call(functools.partial(final_kernel, plan, last), grid=(vectors...  10.1 us
    pallas_call x1, Pallas kernels, shards(): pl.pallas_call(functools.partial(narrow_kernel, plan, chunk), grid=(vecto...  8.87 us
    pallas_call x1, Pallas kernels, shards(): pl.pallas_call(functools.partial(wide_kernel, plan, chunk), grid=(vectors...  1.8 us

profile of v1, /device:TPU:0, one launch (start us, length us, event | category | flops | bytes accessed | tf_op | source)
XLA Modules:
  0.0 48.1 jit_solution(8886143711116015517)
XLA Ops:
  0.0 0.0 copy-start
  0.0 2.2 %copy-done = bf16[64,256,128]{2,1,0:T(8,128)(2,1)S(1)} copy-done((bf16[64,256,128]{2,1,0:T(8,128)(2,1)S(1)}, bf16[64,256,128]{2,1,0:T(8,128)(2,1)}, u32[]{:S(2)}) %copy-start) | copy-done | bytes 4194328
  2.2 0.0 copy-start.2
  2.2 1.2 %copy-done.2 = bf16[8,4,128,128]{3,2,1,0:T(8,128)(2,1)S(1)} copy-done((bf16[8,4,128,128]{3,2,1,0:T(8,128)(2,1)S(1)}, bf16[8,4,128,128]{3,2,1,0:T(8,128)(2,1)}, u32[]{:S(2)}) %copy-start.2) | copy-done | bytes 1048600
  3.4 0.0 copy-start.9
  3.4 0.7 %copy-done.9 = s32[8,256]{1,0:T(8,128)S(1)} copy-done((s32[8,256]{1,0:T(8,128)S(1)}, s32[8,256]{1,0:T(8,128)}, u32[]{:S(2)}) %copy-start.9) | copy-done | bytes 8216
  4.1 0.0 copy-start.5
  4.1 1.8 %wide.1 = (bf16[5,64,128]{2,1,0:T(8,128)(2,1)S(1)}, bf16[2,64,128]{2,1,0:T(8,128)(2,1)S(1)}) custom-call(s32[8,256]{1,0:T(8,128)S(1)} %copy-done.9, bf16[64,256,128]{2,1,0:T(8,128)(2,1)S(1)} %copy-done, bf16[8,512,128]{2,1,0:T(8,128)(2,1)S(1)} %bitcast.1), custom_call_target="tpu_custom_call" | custom-call | tf_op jit(solution)/shard_map/wide/pallas_call | solution.py:281
  5.9 0.0 copy-start.7
  5.9 0.6 %copy-done.7 = bf16[5,64,128]{2,1,0:T(8,128)(2,1)} copy-done((bf16[5,64,128]{2,1,0:T(8,128)(2,1)}, bf16[5,64,128]{2,1,0:T(8,128)(2,1)S(1)}, u32[]{:S(2)}) %copy-start.7) | copy-done | bytes 81944
  6.6 0.0 copy-start.12
  6.6 0.6 %copy-done.12 = bf16[2,64,128]{2,1,0:T(8,128)(2,1)} copy-done((bf16[2,64,128]{2,1,0:T(8,128)(2,1)}, bf16[2,64,128]{2,1,0:T(8,128)(2,1)S(1)}, u32[]{:S(2)}) %copy-start.12) | copy-done | bytes 32792
  7.2 0.0 copy-start.6
  7.2 16.8 %exchange.1 = (bf16[5,64,128]{2,1,0:T(8,128)(2,1)}, bf16[2,64,128]{2,1,0:T(8,128)(2,1)}) custom-call(bf16[5,64,128]{2,1,0:T(8,128)(2,1)} %copy-done.7, bf16[2,64,128]{2,1,0:T(8,128)(2,1)} %copy-done.12), custom_call_target="tpu_custom_call" | custom-call | tf_op jit(solution)/shard_map/exchange/pallas_call | solution.py:303
  24.0 0.0 copy-start.1
  24.0 2.2 %copy-done.1 = bf16[64,256,128]{2,1,0:T(8,128)(2,1)S(1)} copy-done((bf16[64,256,128]{2,1,0:T(8,128)(2,1)S(1)}, bf16[64,256,128]{2,1,0:T(8,128)(2,1)}, u32[]{:S(2)}) %copy-start.1) | copy-done | bytes 4194328
  26.2 0.0 copy-start.3
  26.2 1.2 %copy-done.3 = bf16[8,4,128,128]{3,2,1,0:T(8,128)(2,1)S(1)} copy-done((bf16[8,4,128,128]{3,2,1,0:T(8,128)(2,1)S(1)}, bf16[8,4,128,128]{3,2,1,0:T(8,128)(2,1)}, u32[]{:S(2)}) %copy-start.3) | copy-done | bytes 1048600
  27.4 0.0 copy-start.4
  27.4 0.9 %copy-done.4 = bf16[8,128,128]{2,1,0:T(8,128)(2,1)S(1)} copy-done((bf16[8,128,128]{2,1,0:T(8,128)(2,1)S(1)}, bf16[8,128,128]{2,1,0:T(8,128)(2,1)}, u32[]{:S(2)}) %copy-start.4) | copy-done | bytes 262168
  28.3 0.0 copy-start.10
  28.3 0.7 %copy-done.10 = s32[8,256]{1,0:T(8,128)S(1)} copy-done((s32[8,256]{1,0:T(8,128)S(1)}, s32[8,256]{1,0:T(8,128)}, u32[]{:S(2)}) %copy-start.10) | copy-done | bytes 8216
  29.0 0.0 copy-start.8
  29.0 0.0 copy-start.11
  29.0 8.9 %narrow.1.lifted_ref = bf16[64,384,128]{2,1,0:T(8,128)(2,1)S(1)} custom-call(s32[8,256]{1,0:T(8,128)S(1)} %copy-done.10, bf16[64,256,128]{2,1,0:T(8,128)(2,1)S(1)} %copy-done.1, bf16[8,512,128]{2,1,0:T(8,128)(2,1)S(1)} %bitcast.2, bf16[8,128,128]{2,1,0:T(8,128)(2,1)S(1)} %copy-done.4), custom_call_target="tpu_custom_call" | custom-call | tf_op jit(solution)/shard_map/narrow/pallas_call | solution.py:320
  37.9 0.0 copy-done.5
  37.9 0.0 copy-done.6
  37.9 0.0 copy-done.8
  37.9 0.0 copy-done.11
  38.0 10.1 %final.1 = f32[64,256,128]{2,1,0:T(8,128)} custom-call(s32[8,256]{1,0:T(8,128)S(1)} %copy-done.10, bf16[5,64,128]{2,1,0:T(8,128)(2,1)S(1)} %copy-done.8, bf16[2,64,128]{2,1,0:T(8,128)(2,1)S(1)} %copy-done.11, bf16[3,128,128]{2,1,0:T(8,128)(2,1)S(1)} %copy-done.6, bf16[8,512,128]{2,1,0:T(8,128)(2,1)S(1)} %bitcast.3, bf16[8,128,128]{2,1,0:T(8,128)(2,1)S(1)} %copy-done.5, ...), custom_call_target="tpu_custom_call" | custom-call | tf_op jit(solution)/shard_map/final/pallas_call | solution.py:335
Async XLA Ops:
  0.0 2.2 %copy-start = (bf16[64,256,128]{2,1,0:T(8,128)(2,1)S(1)}, bf16[64,256,128]{2,1,0:T(8,128)(2,1)}, u32[]{:S(2)}) copy-start(bf16[64,256,128]{2,1,0:T(8,128)(2,1)} %fine_ref.5) | copy-start | bytes 12582916
  2.2 1.2 %copy-start.2 = (bf16[8,4,128,128]{3,2,1,0:T(8,128)(2,1)S(1)}, bf16[8,4,128,128]{3,2,1,0:T(8,128)(2,1)}, u32[]{:S(2)}) copy-start(bf16[8,4,128,128]{3,2,1,0:T(8,128)(2,1)} %param.8) | copy-start | bytes 3145732
  3.4 0.7 %copy-start.9 = (s32[8,256]{1,0:T(8,128)S(1)}, s32[8,256]{1,0:T(8,128)}, u32[]{:S(2)}) copy-start(s32[8,256]{1,0:T(8,128)} %pattern_ref.5) | copy-start | bytes 24580
  4.1 33.8 %copy-start.5 = (bf16[8,128,128]{2,1,0:T(8,128)(2,1)S(1)}, bf16[8,128,128]{2,1,0:T(8,128)(2,1)}, u32[]{:S(2)}) copy-start(bf16[8,128,128]{2,1,0:T(8,128)(2,1)} %inverse_ref.3) | copy-start | bytes 786436
  5.9 0.6 %copy-start.7 = (bf16[5,64,128]{2,1,0:T(8,128)(2,1)}, bf16[5,64,128]{2,1,0:T(8,128)(2,1)S(1)}, u32[]{:S(2)}) copy-start(bf16[5,64,128]{2,1,0:T(8,128)(2,1)S(1)} %get-tuple-element.9.coarse_ref) | copy-start | bytes 245764
  6.6 0.6 %copy-start.12 = (bf16[2,64,128]{2,1,0:T(8,128)(2,1)}, bf16[2,64,128]{2,1,0:T(8,128)(2,1)S(1)}, u32[]{:S(2)}) copy-start(bf16[2,64,128]{2,1,0:T(8,128)(2,1)S(1)} %get-tuple-element.10.halo_ref) | copy-start | bytes 98308
  7.2 30.8 %copy-start.6 = (bf16[3,128,128]{2,1,0:T(8,128)(2,1)S(1)}, bf16[3,128,128]{2,1,0:T(8,128)(2,1)}, u32[]{:S(2)}) copy-start(bf16[3,128,128]{2,1,0:T(8,128)(2,1)} %stencil_ref.1) | copy-start | bytes 294916
  24.0 2.2 %copy-start.1 = (bf16[64,256,128]{2,1,0:T(8,128)(2,1)S(1)}, bf16[64,256,128]{2,1,0:T(8,128)(2,1)}, u32[]{:S(2)}) copy-start(bf16[64,256,128]{2,1,0:T(8,128)(2,1)} %fine_ref.5) | copy-start | bytes 12582916
  26.2 1.2 %copy-start.3 = (bf16[8,4,128,128]{3,2,1,0:T(8,128)(2,1)S(1)}, bf16[8,4,128,128]{3,2,1,0:T(8,128)(2,1)}, u32[]{:S(2)}) copy-start(bf16[8,4,128,128]{3,2,1,0:T(8,128)(2,1)} %param.8) | copy-start | bytes 3145732
  27.4 0.9 %copy-start.4 = (bf16[8,128,128]{2,1,0:T(8,128)(2,1)S(1)}, bf16[8,128,128]{2,1,0:T(8,128)(2,1)}, u32[]{:S(2)}) copy-start(bf16[8,128,128]{2,1,0:T(8,128)(2,1)} %inverse_ref.3) | copy-start | bytes 786436
  28.3 0.7 %copy-start.10 = (s32[8,256]{1,0:T(8,128)S(1)}, s32[8,256]{1,0:T(8,128)}, u32[]{:S(2)}) copy-start(s32[8,256]{1,0:T(8,128)} %pattern_ref.5) | copy-start | bytes 24580
  29.0 8.9 %copy-start.8 = (bf16[5,64,128]{2,1,0:T(8,128)(2,1)S(1)}, bf16[5,64,128]{2,1,0:T(8,128)(2,1)}, u32[]{:S(2)}) copy-start(bf16[5,64,128]{2,1,0:T(8,128)(2,1)} %get-tuple-element.11.sums_ref) | copy-start | bytes 245764
  29.0 8.9 %copy-start.11 = (bf16[2,64,128]{2,1,0:T(8,128)(2,1)S(1)}, bf16[2,64,128]{2,1,0:T(8,128)(2,1)}, u32[]{:S(2)}) copy-start(bf16[2,64,128]{2,1,0:T(8,128)(2,1)} %get-tuple-element.12.beside_ref) | copy-start | bytes 98308

commit v2 on v1

v2 whole, which is shorter than its diff:
```python
import functools

import jax
import jax.numpy as jnp
from jax import lax
from jax.experimental import pallas as pl
from jax.experimental.pallas import tpu as pltpu
from jax.sharding import PartitionSpec as P

MESH = pl.DeviceIdType.MESH
F32 = jnp.float32
BF16 = jnp.bfloat16
TILE = 16
VMEM_LIMIT = 63 * 2**20


def round_up(value, unit):
    return -(-value // unit) * unit


class Plan:
    def __init__(self, devices, vectors, blocks, width, levels, kinds):
        self.devices, self.vectors, self.blocks = devices, vectors, blocks
        self.width, self.levels, self.kinds = width, levels, kinds
        all_blocks = devices * blocks
        self.spans, self.local_spans, self.counts, self.groups = [], [], [], []
        for level in range(levels):
            span = all_blocks // max(all_blocks // 4 ** (level + 1), 1)
            local = min(span, blocks)
            self.spans.append(span)
            self.local_spans.append(local)
            self.counts.append(blocks // local)
            self.groups.append(span // local)
        self.narrow = [l for l in range(levels) if self.counts[l] > 1]
        self.wide = [l for l in range(levels) if self.counts[l] == 1]
        self.crossing = [l for l in range(levels) if self.groups[l] > 1]
        self.padded = {l: round_up(self.counts[l], TILE) for l in self.narrow}
        self.offsets, at = {}, 0
        for l in self.narrow:
            self.offsets[l] = at
            at += kinds * self.padded[l]
        self.narrow_rows = at
        self.wide_used = len(self.wide) * kinds + 2
        self.wide_rows = round_up(self.wide_used, TILE)


def wide_rows_onehot(plan, pattern, rows_axis):
    shape = (plan.wide_rows, plan.blocks) if rows_axis == 0 else (plan.blocks, plan.wide_rows)
    row = lax.broadcasted_iota(jnp.int32, shape, rows_axis)
    block = lax.broadcasted_iota(jnp.int32, shape, 1 - rows_axis)
    base = len(plan.wide) * plan.kinds
    hit = ((row == base) & (block == 0)) | ((row == base + 1) & (block == plan.blocks - 1))
    for position, level in enumerate(plan.wide):
        kinds = pattern[level : level + 1, :] if rows_axis == 0 else pattern[:, level : level + 1]
        first = position * plan.kinds
        inside = (row >= first) & (row < first + plan.kinds)
        hit = hit | (inside & (row - first == kinds))
    return hit.astype(F32).astype(BF16)


def narrow_onehot(plan, pattern, level, rows_axis):
    padded = plan.padded[level]
    rows = plan.kinds * padded
    shape = (rows, plan.blocks) if rows_axis == 0 else (plan.blocks, rows)
    row = lax.broadcasted_iota(jnp.int32, shape, rows_axis)
    block = lax.broadcasted_iota(jnp.int32, shape, 1 - rows_axis)
    kinds = pattern[level : level + 1, :] if rows_axis == 0 else pattern[:, level : level + 1]
    target = kinds * padded + block // plan.local_spans[level]
    return (row == target).astype(F32).astype(BF16)


def exchange_kernel(plan, chunk, pattern_ref, fine_hbm, restrict_hbm, inverse_hbm, lifted_hbm, wide_hbm, beside_ref,
                    fine_ref, restrict_ref, inverse_ref, lifted_ref, wide_ref, wide_f32, wide_onehot, onehot, few,
                    grouped, rows, coarse_ref, halo_ref,
                    from_group, to_column, from_column, to_group, back,
                    fine_sem, weight_sem, lifted_sem, wide_sem, group_send, group_recv,
                    column_send, column_recv, back_send, back_recv, halo_send, halo_recv):
    width, kinds = plan.width, plan.kinds
    steps = plan.vectors // chunk
    devices = plan.devices
    near = plan.groups[plan.crossing[0]]
    far = devices // near
    local = len(plan.wide) - len(plan.crossing)
    crossing = len(plan.crossing)
    part = plan.vectors // near
    me = lax.axis_index("gx")
    mine = lax.rem(me, near)
    place = me // near

    def chunk_of(step):
        return pl.ds(pl.multiple_of(step * chunk, chunk), chunk)

    def fine_copy(step):
        return pltpu.make_async_copy(fine_hbm.at[chunk_of(step)], fine_ref.at[chunk_of(step)], fine_sem.at[step])

    def lifted_copy(step):
        return pltpu.make_async_copy(lifted_ref.at[chunk_of(step)], lifted_hbm.at[chunk_of(step)], lifted_sem.at[step])

    weight_copies = [
        pltpu.make_async_copy(restrict_hbm, restrict_ref, weight_sem.at[0]),
        pltpu.make_async_copy(inverse_hbm, inverse_ref, weight_sem.at[1]),
    ]
    for step in range(steps):
        fine_copy(step).start()
    for copy in weight_copies:
        copy.start()

    def group_peer(apart):
        return place * near + lax.rem(mine + apart, near)

    def column_peer(apart):
        return lax.rem(place + apart, far) * near + mine

    nexts = lax.rem(me + 1, devices)
    previous = lax.rem(me + devices - 1, devices)
    barrier = pltpu.get_barrier_semaphore()
    peers = [group_peer(a) for a in range(1, near)] + [column_peer(a) for a in range(1, far)] + [nexts, previous]
    for peer in peers:
        pl.semaphore_signal(barrier, inc=1, device_id=(peer,), device_id_type=MESH)

    wide_onehot[...] = wide_rows_onehot(plan, pattern_ref[...], 0)

    def gather_wide(step, _):
        fine_copy(step).wait()
        here = chunk_of(step)
        for first in range(0, chunk, 2):
            at = step * chunk + first
            both = jnp.concatenate([fine_ref[at], fine_ref[at + 1]], axis=1)
            both = jnp.dot(wide_onehot[...], both, preferred_element_type=F32)
            few[first] = both[:, :width]
            few[first + 1] = both[:, width:]
        for row in range(plan.wide_used):
            rows[row, here, :] = few[:, row, :].astype(BF16)
        return 0

    lax.fori_loop(0, steps, gather_wide, 0)
    for copy in weight_copies:
        copy.wait()
    for position, level in enumerate(plan.wide):
        first = position * kinds
        joined = jnp.concatenate([rows[first + kind] for kind in range(kinds)], axis=1)
        coarse = jnp.dot(joined, restrict_ref[level], preferred_element_type=F32)
        coarse_ref[position] = (coarse * plan.spans[level] ** (-0.5)).astype(BF16)
    base = len(plan.wide) * kinds
    halo_ref[0] = rows[base]
    halo_ref[1] = rows[base + 1]

    pl.semaphore_wait(barrier, len(peers))

    def part_of(index):
        return pl.ds(pl.multiple_of(index * part, part), part)

    copies = []
    for apart in range(1, near):
        theirs = lax.rem(mine + apart, near)
        copies.append(pltpu.make_async_remote_copy(
            src_ref=coarse_ref.at[pl.ds(local, crossing), part_of(theirs), :],
            dst_ref=from_group.at[apart],
            send_sem=group_send.at[apart], recv_sem=group_recv.at[apart],
            device_id=(group_peer(apart),), device_id_type=MESH))
    halo_copies = []
    for side, peer in ((0, previous), (1, nexts)):
        halo_copies.append(pltpu.make_async_remote_copy(
            src_ref=halo_ref.at[side], dst_ref=beside_ref.at[1 - side],
            send_sem=halo_send.at[side], recv_sem=halo_recv.at[1 - side],
            device_id=(peer,), device_id_type=MESH))
    for copy in copies + halo_copies:
        copy.start()

    for level in plan.narrow:
        onehot[pl.ds(plan.offsets[level], kinds * plan.padded[level]), :] = narrow_onehot(
            plan, pattern_ref[...], level, 0)

    def narrow(step, _):
        here = chunk_of(step)
        for first in range(0, chunk, 2):
            at = step * chunk + first
            both = jnp.concatenate([fine_ref[at], fine_ref[at + 1]], axis=1)
            both = jnp.dot(onehot[...], both, preferred_element_type=F32).astype(BF16)
            grouped[first] = both[:, :width]
            grouped[first + 1] = both[:, width:]
        for level in plan.narrow:
            padded = plan.padded[level]
            slices = [pl.ds(plan.offsets[level] + kind * padded, padded) for kind in range(kinds)]
            joined = jnp.concatenate(
                [grouped[:, tile, :].reshape(chunk * padded, width) for tile in slices], axis=1)
            coarse = jnp.dot(joined, restrict_ref[level], preferred_element_type=F32)
            rounded = (coarse * plan.spans[level] ** (-0.5)).astype(BF16)
            solved = jnp.dot(rounded, inverse_ref[level], preferred_element_type=F32).astype(BF16)
            lifted = lax.dot_general(
                solved, restrict_ref[level], (((1,), (1,)), ((), ())), preferred_element_type=F32).astype(BF16)
            for kind, tile in enumerate(slices):
                lifted_ref[here, tile, :] = lifted[:, kind * width : (kind + 1) * width].reshape(chunk, padded, width)
        lifted_copy(step).start()
        return 0

    def lift_wide(position, rounded):
        level = plan.wide[position]
        solved = jnp.dot(rounded, inverse_ref[level], preferred_element_type=F32).astype(BF16)
        lifted = lax.dot_general(
            solved, restrict_ref[level], (((1,), (1,)), ((), ())), preferred_element_type=F32)
        for kind in range(kinds):
            wide_f32[:, position * kinds + kind, :] = lifted[:, kind * width : (kind + 1) * width]

    first_stop = steps // 4
    second_stop = steps - max(steps // 4, 1)
    lax.fori_loop(0, first_stop, narrow, 0)

    total = coarse_ref[pl.ds(local, crossing), part_of(mine), :].astype(F32)
    for apart, copy in enumerate(copies, 1):
        copy.wait_recv()
        total = total + from_group[apart].astype(F32)
    to_column[...] = total.astype(BF16)

    column_copies = []
    for apart in range(1, far):
        column_copies.append(pltpu.make_async_remote_copy(
            src_ref=to_column.at[pl.ds(1, crossing - 1)], dst_ref=from_column.at[apart],
            send_sem=column_send.at[apart], recv_sem=column_recv.at[apart],
            device_id=(column_peer(apart),), device_id_type=MESH))
    for copy in column_copies:
        copy.start()

    for row in range(plan.wide_used, plan.wide_rows):
        wide_f32[:, row, :] = jnp.zeros((plan.vectors, width), F32)
    for position in range(local):
        lift_wide(position, coarse_ref[position])
    lax.fori_loop(first_stop, second_stop, narrow, 0)

    to_group[0] = to_column[0]
    sums = [to_column[index].astype(F32) for index in range(crossing)]
    for apart, copy in enumerate(column_copies, 1):
        copy.wait_recv()
        source = lax.rem(place + far - apart, far)
        for index in range(1, crossing):
            reach = plan.groups[plan.crossing[index]] // near
            keep = (source // reach == place // reach).astype(F32)
            sums[index] = sums[index] + keep * from_column[apart, index - 1].astype(F32)
    for index in range(1, crossing):
        to_group[index] = sums[index].astype(BF16)

    back_copies = []
    for apart in range(1, near):
        back_copies.append(pltpu.make_async_remote_copy(
            src_ref=to_group, dst_ref=back.at[apart],
            send_sem=back_send.at[apart], recv_sem=back_recv.at[apart],
            device_id=(group_peer(apart),), device_id_type=MESH))
    for copy in back_copies:
        copy.start()

    lax.fori_loop(second_stop, steps, narrow, 0)
    for copy in halo_copies:
        copy.wait_recv()
    for copy in copies:
        copy.wait_send()
    coarse_ref[pl.ds(local, crossing), part_of(mine), :] = to_group[...]
    for apart, copy in enumerate(back_copies, 1):
        copy.wait_recv()
        source = lax.rem(mine + near - apart, near)
        coarse_ref[pl.ds(local, crossing), part_of(source), :] = back[apart]
    for position in range(local, len(plan.wide)):
        lift_wide(position, coarse_ref[position])
    wide_ref[...] = wide_f32[...].astype(BF16)
    wide_copy = pltpu.make_async_copy(wide_ref, wide_hbm, wide_sem)
    wide_copy.start()
    for step in range(steps):
        lifted_copy(step).wait()
    for copy in halo_copies + column_copies + back_copies:
        copy.wait_send()
    wide_copy.wait()


def final_kernel(plan, chunk, pattern_ref, beside_ref, stencil_ref,
                 fine_ref, lifted_ref, wide_ref, out_ref, spread, halo, before, after):
    step = pl.program_id(0)
    width, blocks = plan.width, plan.blocks

    @pl.when(step == 0)
    def _():
        turned = pattern_ref[...].T
        for level in plan.narrow:
            columns = pl.ds(plan.offsets[level], plan.kinds * plan.padded[level])
            spread[:, columns] = narrow_onehot(plan, turned, level, 1)
        spread[:, pl.ds(plan.narrow_rows, plan.wide_rows)] = wide_rows_onehot(plan, turned, 1)
        halo[0] = jnp.dot(beside_ref[0], stencil_ref[0], preferred_element_type=F32)
        halo[1] = jnp.dot(beside_ref[1], stencil_ref[2], preferred_element_type=F32)

    stencils = jnp.concatenate([stencil_ref[0], stencil_ref[1], stencil_ref[2]], axis=1)
    for first in range(0, chunk, 2):
        tables = [jnp.concatenate([lifted_ref[first + slot], wide_ref[first + slot]], axis=0) for slot in range(2)]
        both = jnp.dot(spread[...], jnp.concatenate(tables, axis=1), preferred_element_type=F32)
        for slot in range(2):
            vector = pl.ds(step * chunk + first + slot, 1)
            three = jnp.dot(fine_ref[first + slot], stencils, preferred_element_type=F32)
            before[slot, pl.ds(7, 1), :] = halo[0, vector, :]
            before[slot, pl.ds(8, blocks), :] = three[:, :width]
            after[slot, pl.ds(0, blocks), :] = three[:, 2 * width :]
            after[slot, pl.ds(blocks, 1), :] = halo[1, vector, :]
            result = both[:, slot * width : (slot + 1) * width] + three[:, width : 2 * width]
            result = result + before[slot, pl.ds(7, blocks), :]
            out_ref[first + slot] = result + after[slot, pl.ds(1, blocks), :]


def whole(ndim_shape):
    return pl.BlockSpec(ndim_shape, lambda *_: (0,) * len(ndim_shape))


def shards(fine, pattern, stencil, restrict, coarse_inv):
    devices = lax.axis_size("gx")
    vectors, blocks, width = fine.shape
    levels, kinds = restrict.shape[:2]
    plan = Plan(devices, vectors, blocks, width, levels, kinds)
    stacked = restrict.reshape(levels, kinds * width, width)
    wide_count = len(plan.wide)
    params = pltpu.CompilerParams(dimension_semantics=("arbitrary",), vmem_limit_bytes=VMEM_LIMIT)
    chunk = 16
    steps = vectors // chunk
    near = plan.groups[plan.crossing[0]]
    far = devices // near
    crossing = len(plan.crossing)
    part = vectors // near
    vmem = pl.BlockSpec(memory_space=pltpu.VMEM)
    hbm = pl.BlockSpec(memory_space=pl.ANY)
    dma = pltpu.SemaphoreType.DMA
    lifted, wide, beside = pl.pallas_call(
        functools.partial(exchange_kernel, plan, chunk),
        out_shape=(
            jax.ShapeDtypeStruct((vectors, plan.narrow_rows, width), BF16),
            jax.ShapeDtypeStruct((vectors, plan.wide_rows, width), BF16),
            jax.ShapeDtypeStruct((2, vectors, width), BF16),
        ),
        in_specs=[vmem, hbm, hbm, hbm],
        out_specs=(hbm, hbm, vmem),
        scratch_shapes=[
            pltpu.VMEM(fine.shape, BF16),
            pltpu.VMEM(stacked.shape, BF16),
            pltpu.VMEM(coarse_inv.shape, BF16),
            pltpu.VMEM((vectors, plan.narrow_rows, width), BF16),
            pltpu.VMEM((vectors, plan.wide_rows, width), BF16),
            pltpu.VMEM((vectors, plan.wide_rows, width), F32),
            pltpu.VMEM((plan.wide_rows, blocks), BF16),
            pltpu.VMEM((plan.narrow_rows, blocks), BF16),
            pltpu.VMEM((chunk, plan.wide_rows, width), F32),
            pltpu.VMEM((chunk, plan.narrow_rows, width), BF16),
            pltpu.VMEM((plan.wide_used, vectors, width), BF16),
            pltpu.VMEM((wide_count, vectors, width), BF16),
            pltpu.VMEM((2, vectors, width), BF16),
            pltpu.VMEM((near, crossing, part, width), BF16),
            pltpu.VMEM((crossing, part, width), BF16),
            pltpu.VMEM((far, crossing - 1, part, width), BF16),
            pltpu.VMEM((crossing, part, width), BF16),
            pltpu.VMEM((near, crossing, part, width), BF16),
            dma((steps,)), dma((2,)), dma((steps,)), dma,
            dma((near,)), dma((near,)), dma((far,)), dma((far,)), dma((near,)), dma((near,)), dma((2,)), dma((2,)),
        ],
        compiler_params=pltpu.CompilerParams(
            collective_id=0, has_side_effects=True, vmem_limit_bytes=VMEM_LIMIT),
        name="exchange",
    )(pattern, fine, stacked, coarse_inv)

    last = 8
    return pl.pallas_call(
        functools.partial(final_kernel, plan, last),
        grid=(vectors // last,),
        out_shape=jax.ShapeDtypeStruct(fine.shape, F32),
        in_specs=[
            whole(pattern.shape), whole(beside.shape), whole(stencil.shape),
            pl.BlockSpec((last, blocks, width), lambda i: (i, 0, 0)),
            pl.BlockSpec((last, plan.narrow_rows, width), lambda i: (i, 0, 0)),
            pl.BlockSpec((last, plan.wide_rows, width), lambda i: (i, 0, 0)),
        ],
        out_specs=pl.BlockSpec((last, blocks, width), lambda i: (i, 0, 0)),
        scratch_shapes=[
            pltpu.VMEM((blocks, plan.narrow_rows + plan.wide_rows), BF16),
            pltpu.VMEM((2, vectors, width), F32),
            pltpu.VMEM((2, blocks + 8, width), F32),
            pltpu.VMEM((2, blocks + 8, width), F32),
        ],
        compiler_params=params,
        name="final",
    )(pattern, beside, stencil, fine, lifted, wide)


def solution(mesh):
    in_specs = (P(None, "gx", None), P(None, "gx"), P(), P(), P())
    out_specs = P(None, "gx", None)
    return jax.shard_map(shards, mesh=mesh, in_specs=in_specs, out_specs=out_specs, check_vma=False)
```

time: 48.5 us -> 33.9 us (0.70)
  local copies, waits for them, and re-layouts: 10.4 us -> 0 us
  Pallas kernels: 37.6 us -> 33.5 us
    unnamed x26 -> x0, local copies, waits for them, and re-layouts: 10.4 us -> none
    pallas_call x3 -> x1, Pallas kernels: 27.5 us -> 20.3 us  [shards(): pl.pallas_call(functools.partial(exchange_kernel, plan, chunk), out_shape...]
    pallas_call x1, Pallas kernels: 10.1 us -> 13.2 us  [shards(): pl.pallas_call(functools.partial(final_kernel, plan, last), grid=(vectors...]
where the time goes in v2:
time: 33.9 us; the launch traced here: 33.5 us
  Pallas kernels  33.5 us (99%)
    pallas_call x1, Pallas kernels, shards(): pl.pallas_call(functools.partial(exchange_kernel, plan, chunk), out_shape...  20.3 us
    pallas_call x1, Pallas kernels, shards(): pl.pallas_call(functools.partial(final_kernel, plan, last), grid=(vectors...  13.2 us

profile of v2, /device:TPU:0, one launch (start us, length us, event | category | flops | bytes accessed | tf_op | source)
XLA Modules:
  0.0 33.5 jit_solution(3395085588204491096)
XLA Ops:
  0.0 20.3 %exchange.1 = (bf16[64,384,128]{2,1,0:T(8,128)(2,1)}, bf16[64,32,128]{2,1,0:T(8,128)(2,1)}, bf16[2,64,128]{2,1,0:T(8,128)(2,1)}) custom-call(s32[8,256]{1,0:T(8,128)} %pattern_ref.3, bf16[64,256,128]{2,1,0:T(8,128)(2,1)} %fine_ref.1, bf16[8,512,128]{2,1,0:T(8,128)(2,1)} %bitcast.1, bf16[8,128,128]{2,1,0:T(8,128)(2,1)} %inverse_hbm.1), custom_call_target="tpu_custom_call" | custom-call | tf_op jit(solution)/shard_map/exchange/pallas_call | solution.py:325
  20.3 13.2 %final.1 = f32[64,256,128]{2,1,0:T(8,128)} custom-call(s32[8,256]{1,0:T(8,128)} %pattern_ref.3, bf16[2,64,128]{2,1,0:T(8,128)(2,1)} %get-tuple-element.8.beside_ref, bf16[3,128,128]{2,1,0:T(8,128)(2,1)} %stencil_ref.1, bf16[64,256,128]{2,1,0:T(8,128)(2,1)} %fine_ref.1, bf16[64,384,128]{2,1,0:T(8,128)(2,1)} %get-tuple-element.9.lifted_ref, ...), custom_call_target="tpu_custom_call" | custom-call | tf_op jit(solution)/shard_map/final/pallas_call | solution.py:362
